TPU v7x, 32 devices: a whole 2x2x4 slice. The times are simulated.
32 devices in a mesh: g: 32 (over z, y, x, core).
Axes of the slice: x: 2, y: 2, z: 4, core: 2. Of those that a mesh axis runs over, the one named last changes fastest.
Arguments:
- features: bfloat16 [65536, 128], P(None, 'g')
- w_self1: bfloat16 [128, 128], P('g')
- w_nbr1: bfloat16 [128, 128], P('g')
- nbr_ids: int32 [65536, 10], P('g')
- nbr_mask: int32 [65536, 10], P('g')
- w_self2: bfloat16 [128, 128], replicated
- w_nbr2: bfloat16 [128, 128], replicated
- w_self3: bfloat16 [128, 40], replicated
- w_nbr3: bfloat16 [128, 40], replicated
- labels: int32 [65536], P('g')
Outputs:
- output 1: float32 [], replicated
- output 2: float32 [128, 128], P('g')
- output 3: float32 [128, 128], P('g')
- output 4: float32 [128, 128], replicated
- output 5: float32 [128, 128], replicated
- output 6: float32 [128, 40], replicated
- output 7: float32 [128, 40], replicated
All inputs are finite; a program needn't handle non-finite values.
Results may differ from a plain program's by a relative error of at most 0.00265331.
Values are sent between devices in bfloat16 or wider.
A program may use at most 1 GiB of HBM per device.

v0:
```python
import jax
import jax.numpy as jnp
from jax import lax
from jax.experimental import pallas as pl
from jax.experimental.pallas import tpu as pltpu
from jax.sharding import PartitionSpec as P


AX = 'g'
N = 65536
R = 2048
D = 128
K = 10
C = 40
NDEV = 32
E = R * K
CAP = 2048
NACC = 8
EDGES = 64
SLOTS = 8
TBUF = 10
BBUF = 8
UNROLL = 32
MESH = pl.DeviceIdType.MESH
VMEM = pltpu.VMEM
BF = jnp.bfloat16
F32 = jnp.float32
VLIM = 62 * 1024 * 1024
LLIM = 46 * 1024 * 1024
GLIM = 48 * 1024 * 1024


def gather_blocks(arrays, chunks, order, lsem, rsem, sems):
    nq = len(chunks)
    me = lax.axis_index(AX)
    z, y, x, c = me // 8, lax.rem(me // 4, 2), lax.rem(me // 2, 2), lax.rem(me, 2)

    def dev(z_, y_, x_, c_):
        return ((z_ * 2 + y_) * 2 + x_) * 2 + c_

    d_x, d_y, d_up, d_dn, d_c = dev(z, y, 1 - x, c), dev(z, 1 - y, x, c), me + 8, me - 8, dev(z, y, x, 1 - c)
    bar = pltpu.get_barrier_semaphore()
    for d in (d_x, d_y, d_c):
        pl.semaphore_signal(bar, device_id=(d,), device_id_type=MESH)

    @pl.when(z < 3)
    def _():
        pl.semaphore_signal(bar, device_id=(d_up,), device_id_type=MESH)

    @pl.when(z > 0)
    def _():
        pl.semaphore_signal(bar, device_id=(d_dn,), device_id_type=MESH)

    pl.semaphore_wait(bar, 4 + lax.rem(z + 1, 4) // 2)
    sent = [[[0] for _ in range(4)] for _ in arrays]

    def place(q, zo, yo, xo):
        array, first, rows, _ = chunks[q]
        block, table = arrays[array]
        return table.at[pl.ds(pl.multiple_of(dev(zo, yo, xo, c) * block.shape[0] + first, 8), rows)]

    def slot(q, zo, yo, xo):
        return rsem.at[((zo * 2 + yo) * 2 + xo) * nq + q]

    def forward(q, zo, yo, xo, up, dn, to_x, to_y, src=None):
        dst = place(q, zo, yo, xo)
        src = dst if src is None else src
        ssem, csem = sems[chunks[q][0]]

        def send(d, ss, rs):
            pltpu.make_async_remote_copy(
                src_ref=src, dst_ref=dst, send_sem=ss, recv_sem=rs, device_id=(d,), device_id_type=MESH).start()

        if up is not None:
            @pl.when(up)
            def _():
                send(d_up, ssem.at[0], slot(q, zo, yo, xo))

            @pl.when(dn)
            def _():
                send(d_dn, ssem.at[1], slot(q, zo, yo, xo))
        for there, d, j in ((to_x, d_x, 2), (to_y, d_y, 3)):
            if there:
                send(d, ssem.at[j], slot(q, zo, yo, xo))
                sent[chunks[q][0]][j][0] += chunks[q][2]
        send(d_c, csem.at[0], csem.at[1])

    own = []
    for q in order[:nq]:
        array, first, rows, _ = chunks[q]
        forward(q, z, y, x, z < 3, z > 0, True, True, arrays[array][0].at[pl.ds(first, rows)])
    for j, (block, table) in enumerate(arrays):
        rb = block.shape[0]
        own.append(pltpu.make_async_copy(block, table.at[pl.ds(pl.multiple_of(me * rb, 8), rb)], lsem.at[j]))
        own[j].start()
    zr = [z, z + 1 - 2 * lax.rem(z, 2), 2 - z // 2, 3 - 3 * (z // 2)]

    for code in order[nq:]:
        kind, r, q = code // 100, code // 10 % 10, code % 10
        plane_first = chunks[q][3]
        zo, yo, xo = zr[r], 1 - y if kind >= 2 else y, 1 - x if kind % 2 else x
        here = place(q, zo, yo, xo)
        pltpu.make_async_remote_copy(
            src_ref=here, dst_ref=here, send_sem=sems[0][0].at[0], recv_sem=slot(q, zo, yo, xo),
            device_id=(d_x,), device_id_type=MESH).wait_recv()
        up = dn = None
        if kind == 0 or plane_first:
            up, dn = (z < 3, z > 0) if r == 0 else ((zo < z) & (z < 3), (zo > z) & (z > 0))
        column = kind == 0 and not plane_first
        across = not plane_first or r == 0
        forward(q, zo, yo, xo, up, dn,
                column or (kind == 2 and q % 2 == 1 and across), column or (kind == 1 and q % 2 == 0 and across))

    for j, (block, table) in enumerate(arrays):
        ssem, csem = sems[j]

        def wait_rows(n, sem, table=table):
            v = table.at[pl.ds(0, n)]
            pltpu.make_async_copy(v, v, sem).wait()

        own[j].wait()
        for k in (2, 3):
            wait_rows(sent[j][k][0], ssem.at[k])
        step = sum(rows * (4 if plane_first else 1) for array, _, rows, plane_first in chunks if array == j)
        for k in range(3):
            @pl.when(z == k)
            def _(k=k):
                wait_rows((k + 1) * step, ssem.at[0])

            @pl.when(z == 3 - k)
            def _(k=k):
                wait_rows((k + 1) * step, ssem.at[1])
        wait_rows(16 * block.shape[0], csem.at[0])
        wait_rows(16 * block.shape[0], csem.at[1])


def cut(*sizes, array=0, plane_first=0):
    return [(array, sum(sizes[:i]), n, i < plane_first) for i, n in enumerate(sizes)]


def steps(*words):
    every = [w // 1000 ** i % 1000 for w in words for i in reversed(range(8))]
    return [v for v in every if v != 999]


ROW_CHUNKS = cut(224, 224, 272, 272, 272, 272, 256, 256, plane_first=2)
ROW_ORDER = steps(
    2003006005000004001007, 14100013201206200204016, 12017027023207101116026, 25015036111032033034211,
    24035021213020115215106, 300110022037220125126205, 104225320113112316120136, 224102217130310203011124,
    301227234114235105132237, 135307313212122010236117, 31134210107123216315121, 202223131103127306321311,
    304030317233133222312232, 137221231326331226230302, 303214305330336332322333, 323337325335314327334324)
PACKED_CHUNKS = cut(144, 144, 128, 128, 128, 128, 112, 112, plane_first=2) + cut(88, 80, array=1)
PACKED_TURNS = [8, 9, *range(8)]
PACKED_ORDER = PACKED_TURNS + [
    kind * 100 + (s + step) * 10 + q for s in range(5) for q in PACKED_TURNS
    for kind, step in ((0, 1), (1, 0), (2, 0), (3, -1)) if 0 <= s + step <= 3]


def all_gather(blocks, chunks, order, cid, limit):
    n = len(blocks)

    def kernel(*refs):
        lsem, rsem, *sems = refs[2 * n:]
        gather_blocks(list(zip(refs[:n], refs[n:2 * n])), chunks, order, lsem, rsem, list(zip(sems[::2], sems[1::2])))

    dma = pltpu.SemaphoreType.DMA
    return pl.pallas_call(
        kernel, out_shape=[jax.ShapeDtypeStruct((v.shape[0] * NDEV,) + v.shape[1:], v.dtype) for v in blocks],
        in_specs=[pl.BlockSpec(memory_space=VMEM)] * n, out_specs=[pl.BlockSpec(memory_space=pltpu.HBM)] * n,
        scratch_shapes=[dma((n,)), dma((16 * len(chunks),))] + [dma((4,)), dma((2,))] * n,
        compiler_params=pltpu.CompilerParams(
            collective_id=cid, has_side_effects=True, vmem_limit_bytes=limit))(*blocks)


def gather_rows(v):
    return all_gather([v], ROW_CHUNKS, ROW_ORDER, 2, GLIM)[0]


def dot(a, b):
    return jnp.dot(a, b, preferred_element_type=F32)


def dot_rows(a, b):
    return lax.dot_general(a, b, (((0,), (0,)), ((), ())), preferred_element_type=F32)


def dot_t(a, b):
    return lax.dot_general(a, b, (((1,), (1,)), ((), ())), preferred_element_type=F32)


CB = 256


def load_table(sources, make, meanwhile=None):
    slots = sources[0][1].shape[0]

    def copies(i, slot):
        for table, space, sem in sources:
            n = space.shape[1]
            rows = table.at[pl.ds(pl.multiple_of(i * n, n), n), :]
            yield pltpu.make_async_copy(rows, space.at[slot], sem.at[slot])

    for i in range(slots - 1):
        for copy in copies(i, i):
            copy.start()
    if meanwhile is not None:
        meanwhile()

    def step(i, _):
        slot = lax.rem(i, slots)
        for copy in copies(i, slot):
            copy.wait()

        @pl.when(i + slots - 1 < NDEV)
        def _():
            for copy in copies(i + slots - 1, lax.rem(i + slots - 1, slots)):
                copy.start()

        make(i, slot)
        return 0

    lax.fori_loop(0, NDEV, step, 0)


class Inputs:
    def __init__(self, operands, spaces, sem):
        self.copies = [pltpu.make_async_copy(a, b, sem.at[j]) for j, (a, b) in enumerate(zip(operands, spaces))]

    def start(self):
        for copy in self.copies:
            copy.start()


def table_mean(tab_hbm, inputs, idx_ref, tab, stg, acc, tsem):
    def widen(i, slot):
        tab[pl.ds(pl.multiple_of(i * R, R), R), :] = stg[slot].astype(F32)

    load_table([(tab_hbm, stg, tsem)], widen, inputs.start)
    tab[pl.ds(N, 8), :] = jnp.zeros((8, D), F32)
    inputs.copies[0].wait()
    slots = [idx_ref.at[pl.ds(k * R, R)] for k in range(K)]

    def body(b, _):
        for u in range(UNROLL):
            r = b * UNROLL + u
            acc[pl.ds(r, 1), :] = total([tab[pl.ds(ids[r], 1), :] for ids in slots])
        return 0

    lax.fori_loop(0, R // UNROLL, body, 0)
    for copy in inputs.copies[1:]:
        copy.wait()


TABLE = [VMEM((N + 8, D), F32), VMEM((TBUF, R, D), BF), VMEM((R, D), F32), pltpu.SemaphoreType.DMA((TBUF,)),
         pltpu.SMEM((E,), jnp.int32), VMEM((R, D), BF), VMEM((R, 2), F32), pltpu.SemaphoreType.DMA((3,))]
HBM = pl.BlockSpec(memory_space=pltpu.HBM)


def hidden_layer(v, idx, side, w_self, w_nbr):
    def kernel(idx_hbm, tab_hbm, x_hbm, side_hbm, ws_ref, wn_ref, agg_ref, pre_ref, act_ref,
               tab, stg, acc, tsem, idx_ref, x_ref, side_ref, sem):
        inputs = Inputs((idx_hbm, x_hbm, side_hbm), (idx_ref, x_ref, side_ref), sem)
        table_mean(tab_hbm, inputs, idx_ref, tab, stg, acc, tsem)

        def block(i, _):
            r = pl.ds(pl.multiple_of(i * CB, CB), CB)
            agg = (acc[r, :] / side_ref[r, :1]).astype(BF)
            agg_ref[r, :] = agg
            pre = dot(x_ref[r, :], ws_ref[...]) + dot(agg, wn_ref[...])
            pre_ref[r, :] = pre
            act_ref[r, :] = jnp.maximum(pre, 0.0).astype(BF)
            return 0

        lax.fori_loop(0, R // CB, block, 0)

    vm = pl.BlockSpec(memory_space=VMEM)
    return pl.pallas_call(
        kernel,
        out_shape=[jax.ShapeDtypeStruct((R, D), BF), jax.ShapeDtypeStruct((R, D), F32), jax.ShapeDtypeStruct((R, D), BF)],
        in_specs=[HBM] * 4 + [vm] * 2,
        out_specs=[vm] * 3, scratch_shapes=TABLE, compiler_params=pltpu.CompilerParams(vmem_limit_bytes=LLIM),
    )(idx, gather_rows(v), v, side, w_self, w_nbr)


HALF = R // 2


def output_layer(v, idx, side, w_self, w_nbr):
    def kernel(idx_hbm, tab_hbm, x_hbm, side_hbm, ws_ref, wn_ref, g_ref, dws_ref, dwn_ref, loss_ref,
               tab, stg, acc, tsem, idx_ref, x_ref, side_ref, sem):
        inputs = Inputs((idx_hbm, x_hbm, side_hbm), (idx_ref, x_ref, side_ref), sem)
        table_mean(tab_hbm, inputs, idx_ref, tab, stg, acc, tsem)
        dws_ref[...] = jnp.zeros((D, D), F32)
        dwn_ref[...] = jnp.zeros((D, D), F32)
        lane = lax.broadcasted_iota(jnp.int32, (CB, D), 1)

        def part(start, half):
            r = pl.ds(pl.multiple_of(start, CB), CB)
            act = x_ref[r, :]
            agg = (acc[r, :] / side_ref[r, :1]).astype(BF)
            logits = dot(act, ws_ref[half]) + dot(agg, wn_ref[half])
            col = lane - half * (D // 2)
            live = (col >= 0) & (col < C)
            top = jnp.max(jnp.where(live, logits, -jnp.inf), axis=1, keepdims=True)
            ex = jnp.where(live, jnp.exp(logits - top), 0.0)
            norm = top + jnp.log(jnp.sum(ex, axis=1, keepdims=True))
            hot = jnp.where(col.astype(F32) == side_ref[r, 1:], 1.0, 0.0)
            loss = jnp.sum(jnp.where(live, hot * (norm - logits), 0.0))
            prob = jnp.where(live, jnp.exp(logits - norm), 0.0)
            g = ((prob - hot) / N).astype(BF)
            dws_ref[...] += dot_rows(act, g)
            dwn_ref[...] += dot_rows(agg, g)
            rest = 1.0 / side_ref[r, :1]
            for j in range(3):
                most = rest.astype(BF)
                g = jnp.where(col == C + j, most, g)
                rest = rest - most.astype(F32)
            return g, loss

        def block(i, loss):
            g_low, loss_low = part(i * CB, 0)
            g_high, loss_high = part(i * CB + HALF, 1)
            g_ref[pl.ds(pl.multiple_of(i * CB, CB), CB), :] = jnp.where(lane < D // 2, g_low, g_high)
            return loss + loss_low + loss_high

        loss = lax.fori_loop(0, HALF // CB, block, jnp.float32(0.0))
        loss_ref[...] = jnp.full((8, D), loss, F32)

    vm = pl.BlockSpec(memory_space=VMEM)
    return pl.pallas_call(
        kernel,
        out_shape=[jax.ShapeDtypeStruct((HALF, D), BF), jax.ShapeDtypeStruct((D, D), F32),
                   jax.ShapeDtypeStruct((D, D), F32), jax.ShapeDtypeStruct((8, D), F32)],
        in_specs=[HBM] * 4 + [vm] * 2,
        out_specs=[vm] * 4, scratch_shapes=TABLE, compiler_params=pltpu.CompilerParams(vmem_limit_bytes=LLIM),
    )(idx, gather_rows(v), v, side, w_self, w_nbr)


def table_mean_t(fetch, marks, lists_hbm, lists, lsem, tab, accs, load, inputs):
    me = lax.axis_index(AX)

    def base_of(s):
        return jnp.minimum(marks[s, me] // 1024, (SPAN - CAP) // 1024) * 1024

    def list_copies(s, part, slot):
        off = pl.multiple_of(s * SPAN + base_of(s) + part * CAP, 1024)
        return [pltpu.make_async_copy(h.at[pl.ds(off, CAP)], b.at[pl.ds(pl.multiple_of(slot * CAP, CAP), CAP)], lsem.at[j, slot])
                for j, (h, b) in enumerate(zip(lists_hbm, lists))]

    def clear():
        inputs.start()
        for a in accs:
            a[...] = jnp.zeros(a.shape, F32)
        fetch.wait()
        for s in range(SLOTS - 1):
            for cp in list_copies(s, 0, s):
                cp.start()

    load(clear)
    src, dst = [[v.at[pl.ds(u, SLOTS * CAP - EDGES + 1)] for u in range(EDGES)] for v in lists]

    def run(slot, first, last):
        def body(b, _):
            e = slot * CAP + b * EDGES
            for u in range(EDGES):
                d = pl.ds(dst[u][e], 1)
                accs[u % NACC][d, :] += tab[pl.ds(src[u][e], 1), :]
            return 0

        lax.fori_loop(first // EDGES, (last + EDGES - 1) // EDGES, body, 0)

    def sender(s, _):
        slot = lax.rem(s, SLOTS)
        for cp in list_copies(s, 0, slot):
            cp.wait()

        @pl.when(s + SLOTS - 1 < NDEV)
        def _():
            for cp in list_copies(s + SLOTS - 1, 0, lax.rem(s + SLOTS - 1, SLOTS)):
                cp.start()

        base = base_of(s)
        end = marks[s, me + 1] - base
        run(slot, marks[s, me] - base, jnp.minimum(end, CAP))

        def more(p, _):
            for cp in list_copies(s, p, slot):
                cp.start()
            for cp in list_copies(s, p, slot):
                cp.wait()
            run(slot, 0, jnp.minimum(end - p * CAP, CAP))
            return 0

        lax.fori_loop(1, (end + CAP - 1) // CAP, more, 0)
        return 0

    lax.fori_loop(0, NDEV, sender, 0)
    for copy in inputs.copies:
        copy.wait()


def backward_layer(packed, table, edges, lists, g_up, w_self, pre, act, agg, w_nbr, w_up):
    last = table is not None

    def kernel(edges_hbm, src_hbm, dst_hbm, packed_hbm, gu_hbm, pre_hbm, act_hbm, agg_hbm, ws_ref, *rest):
        if last:
            table_hbm, dws_ref, dwn_ref = rest[:3]
            rest = rest[3:]
        else:
            wn_ref, wu_ref, g_ref, u_ref, dws_ref, dwn_ref = rest[:6]
            rest = rest[6:]
        accs, rest = rest[:NACC], rest[NACC:]
        marks, src, dst, lsem, tab, spread, gu_ref, pre_ref, act_ref, agg_ref, sem, pstg, psem, *rest = rest
        inputs = Inputs((gu_hbm, pre_hbm, act_hbm, agg_hbm), (gu_ref, pre_ref, act_ref, agg_ref), sem)
        fetch = pltpu.make_async_copy(edges_hbm.at[:, E // D, :], marks, sem.at[4])
        fetch.start()

        part_row = lax.broadcasted_iota(jnp.int32, (D, 2 * D), 0) - C
        part_row -= jnp.where(lax.broadcasted_iota(jnp.int32, (D, 2 * D), 1) < D, 0, D // 2)
        spread[...] = jnp.where((part_row >= 0) & (part_row < 3), 1.0, 0.0).astype(BF)

        def make(i, slot):
            for q in range(HALF // CB):
                part = pstg[slot, q * CB:(q + 1) * CB, :]
                scale = dot(part, spread[...])
                if not last:
                    v = dot(part, wu_ref[...]).astype(BF)
                for half in range(2):
                    at = half * HALF + q * CB
                    lanes = slice(half * D, (half + 1) * D)
                    term = rest[0][slot, at:at + CB, :] if last else v[:, lanes]
                    tab[pl.ds(pl.multiple_of(i * R + at, CB), CB), :] = term.astype(F32) * scale[:, lanes]

        sources = [(packed_hbm, pstg, psem)] + ([(table_hbm, *rest)] if last else [])
        table_mean_t(fetch, marks, (src_hbm, dst_hbm), (src, dst), lsem, tab, accs,
                     lambda clear: load_table(sources, make, clear), inputs)
        dws_ref[...] = jnp.zeros((D, D), F32)
        dwn_ref[...] = jnp.zeros((D, D), F32)

        def part(start, up):
            r = pl.ds(pl.multiple_of(start, CB), CB)
            g = jnp.where(pre_ref[r, :] > 0, up + total([a[r, :] for a in accs]), 0.0).astype(BF)
            dws_ref[...] += dot_rows(act_ref[r, :], g)
            dwn_ref[...] += dot_rows(agg_ref[r, :], g)
            if not last:
                g_ref[r, :] = g
                u_ref[r, :] = dot_t(g, wn_ref[...]).astype(BF)

        def block(i, _):
            if last:
                part(i * CB, dot_t(gu_ref[pl.ds(pl.multiple_of(i * CB, CB), CB), :], ws_ref[...]))
            else:
                gu = gu_ref[pl.ds(pl.multiple_of(i * CB, CB), CB), :]
                part(i * CB, dot_t(gu, ws_ref[0]))
                part(i * CB + HALF, dot_t(gu, ws_ref[1]))
            return 0

        lax.fori_loop(0, (R if last else HALF) // CB, block, 0)

    vm = pl.BlockSpec(memory_space=VMEM)
    outs = [jax.ShapeDtypeStruct((D, D), F32)] * 2
    args = [edges.reshape(NDEV, SPAN // D, D), *lists, packed, g_up, pre, act, agg, w_self]
    specs = [HBM] * 8 + [vm]
    stage = [VMEM((BBUF, HALF, D), BF), pltpu.SemaphoreType.DMA((BBUF,))]
    if last:
        args.append(table)
        specs.append(HBM)
        stage += [VMEM((BBUF, R, D), BF), pltpu.SemaphoreType.DMA((BBUF,))]
    else:
        outs = [jax.ShapeDtypeStruct((R, D), BF)] * 2 + outs
        args += [w_nbr, w_up]
        specs += [vm, vm]
    return pl.pallas_call(
        kernel, out_shape=outs, in_specs=specs, out_specs=[vm] * len(outs),
        scratch_shapes=[VMEM((R + 8, D), F32)] * NACC + [pltpu.SMEM((NDEV, D), jnp.int32)] + [pltpu.SMEM((SLOTS * CAP,), jnp.int32)] * 2
        + [pltpu.SemaphoreType.DMA((2, SLOTS)), VMEM((N, D), F32), VMEM((D, 2 * D), BF)]
        + [VMEM(v.shape, v.dtype) for v in (g_up, pre, act, agg)] + [pltpu.SemaphoreType.DMA((5,))] + stage,
        compiler_params=pltpu.CompilerParams(vmem_limit_bytes=VLIM))(*args)


def rank(j):
    return ((j >> 7) & (NDEV - 1)) * R + (j >> 12) * 128 + (j & 127)


SPAN = 21 * 1024


def sorted_edges(ids, live):
    here = jnp.arange(R, dtype=jnp.int32)[None, :]
    key = jnp.where(live, ids * R + here, -1)
    key = lax.sort(key.reshape(E))
    bounds = jnp.arange(NDEV + 1, dtype=jnp.int32)
    starts = jnp.sum(((key >> 22)[None, :] < bounds[:, None]).astype(jnp.int32), axis=1)
    return jnp.concatenate([key.reshape(E // D, D), jnp.pad(starts[None, :], ((0, 7), (0, D - NDEV - 1)))])


def in_edges(every):
    me = lax.axis_index(AX)
    keys = every.reshape(NDEV, SPAN // D, D)
    sender = jnp.arange(NDEV, dtype=jnp.int32)[:, None, None]
    src = rank(sender * R + (keys & (R - 1)))
    dst = (keys >> 11) - me * R
    real = (dst >= 0) & (dst < R) & (keys >= 0) & (jnp.arange(SPAN // D)[None, :, None] < E // D)
    dst = jnp.where(real, dst, R)
    return src.reshape(-1), dst.reshape(-1)


RED = 24


def total(v):
    while len(v) > 1:
        v = [v[j] + v[j + 1] if j + 1 < len(v) else v[j] for j in range(0, len(v), 2)]
    return v[0]


def reduce_shares(grads, loss, cid):
    n = len(grads)
    step = D // NDEV
    kept, told = pl.ds(0, 2 * step), pl.ds(2 * step, RED - 2 * step)

    def kernel(*refs):
        loss_ref, own_ref, all_ref, p_ref, got, mine, rsem, ssem, lsem = refs[n:]
        for d in range(NDEV):
            for j in range(n):
                p_ref[d, j * step:(j + 1) * step, :] = refs[j][d * step:(d + 1) * step, :]
            p_ref[d, n * step:, :] = loss_ref[:step, :]
        me = lax.axis_index(AX)
        bar = pltpu.get_barrier_semaphore()

        def to_others(do):
            def one(k, _):
                do(lax.rem(me + k, NDEV))
                return 0

            lax.fori_loop(1, NDEV, one, 0)

        def scatter(src_of, dst, j):
            to_others(lambda d: pltpu.make_async_remote_copy(
                src_ref=src_of(d), dst_ref=dst, send_sem=ssem.at[j], recv_sem=rsem.at[j],
                device_id=(d,), device_id_type=MESH).start())

        def drain(v, *done):
            for sem in done:
                pltpu.make_async_copy(v, v, sem).wait()

        to_others(lambda d: pl.semaphore_signal(bar, device_id=(d,), device_id_type=MESH))
        pl.semaphore_wait(bar, NDEV - 1)
        others = pl.ds(0, NDEV - 1)
        scatter(lambda d: p_ref.at[d, told], got.at[me, told], 0)
        scatter(lambda d: p_ref.at[d, kept], got.at[me, kept], 1)
        own = pltpu.make_async_copy(p_ref.at[me], got.at[me], lsem.at[0])
        own.start()
        own.wait()
        drain(got.at[others, told], rsem.at[0])
        mine[...] = total([got[d, told] for d in range(NDEV)])
        drain(got.at[others, told], ssem.at[0])
        scatter(lambda d: mine, all_ref.at[me], 2)
        keep = pltpu.make_async_copy(mine, all_ref.at[me], lsem.at[1])
        keep.start()
        keep.wait()
        drain(got.at[others, kept], rsem.at[1], ssem.at[1])
        own_ref[...] = total([got[d, kept] for d in range(NDEV)])
        drain(all_ref.at[others], rsem.at[2], ssem.at[2])

    dma = pltpu.SemaphoreType.DMA
    vm = pl.BlockSpec(memory_space=VMEM)
    told_rows = jax.ShapeDtypeStruct((NDEV, told.size, D), F32)
    return pl.pallas_call(
        kernel, name='reduce_shares',
        out_shape=[jax.ShapeDtypeStruct((kept.size, D), F32), told_rows],
        in_specs=[vm] * (n + 1), out_specs=[vm, vm],
        scratch_shapes=[VMEM((NDEV, RED, D), F32)] * 2 + [VMEM((told.size, D), F32), dma((3,)), dma((3,)), dma((2,))],
        compiler_params=pltpu.CompilerParams(collective_id=cid, has_side_effects=True))(*grads, loss)


def lay_out(own, every):
    step = D // NDEV

    def kernel(own_ref, all_ref, loss_ref, self1, nbr1, self2, nbr2, self3, nbr3, last):
        self1[...], nbr1[...] = own_ref[:step, :], own_ref[step:, :]
        for d in range(NDEV):
            for j, out in enumerate((self2, nbr2, last)):
                out[d * step:(d + 1) * step, :] = all_ref[d, j * step:(j + 1) * step, :]
        turned = last[...].T
        self3[...], nbr3[...] = turned[:C], turned[D // 2:D // 2 + C]
        loss_ref[...] = all_ref[0, 3 * step:3 * step + 1, :1] / N

    shapes = [(1, 1), (step, D), (step, D), (D, D), (D, D), (C, D), (C, D)]
    return pl.pallas_call(
        kernel, name='lay_out', out_shape=[jax.ShapeDtypeStruct(v, F32) for v in shapes],
        scratch_shapes=[VMEM((D, D), F32)])(own, every)


def solution(mesh):
    def device_step(feat_cols, w_self1_rows, w_nbr1_rows, nbr_rows, mask_rows, w_self2, w_nbr2, w_self3, w_nbr3, label_rows):
        me = lax.axis_index(AX)
        live = mask_rows.T > 0
        ids = rank(nbr_rows.T)
        w1_rows = jnp.concatenate([w_self1_rows, w_nbr1_rows], axis=1)
        out_going = jnp.concatenate(
            [feat_cols.T.reshape(4, 16, NDEV, 128).transpose(2, 0, 1, 3).reshape(NDEV, 4, R),
             jnp.broadcast_to(w1_rows[None], (NDEV, 4, 2 * D))], axis=2)
        in_coming = lax.all_to_all(out_going, AX, 0, 0, tiled=True)
        edges = sorted_edges(ids, live)
        rows = jnp.concatenate([jnp.where(live, ids, N), label_rows[None, :], jnp.zeros((5, R), jnp.int32)])
        blocks = rows.reshape(16, 16, 128).transpose(1, 0, 2)
        blocks = lax.all_to_all(jnp.concatenate([blocks, blocks]), AX, 0, 0, tiled=True)
        rows = lax.dynamic_index_in_dim(blocks.reshape(16, 2, 16, 128), me // 16, 1, keepdims=False)
        rows = rows.transpose(1, 0, 2).reshape(16, R)
        idx, labels = rows[:K], rows[K]
        in_coming = in_coming.reshape(D, R + 2 * D)
        feat = in_coming[:, :R].T
        w_self1, w_nbr1 = in_coming[:, R:R + D], in_coming[:, R + D:]
        deg = jnp.sum((idx < N).astype(F32), axis=0)
        side = jnp.stack([deg, labels.astype(F32)], axis=1)
        idx = idx.reshape(E)
        halves = lambda w: jnp.stack([jnp.pad(w, ((0, 0), (0, D - C))), jnp.pad(w, ((0, 0), (D // 2, D // 2 - C)))])
        ws3, wn3 = halves(w_self3), halves(w_nbr3)
        wn3_t = jnp.concatenate([wn3[0], wn3[1]]).T
        agg_x, pre_one, act_one = hidden_layer(feat, idx, side, w_self1, w_nbr1)
        agg_one, pre_two, act_two = hidden_layer(act_one, idx, side, w_self2, w_nbr2)
        g_three, dws3, dwn3, loss = output_layer(act_two, idx, side, ws3, wn3)
        packed, edges = all_gather([g_three, edges], PACKED_CHUNKS, PACKED_ORDER, 5, VLIM)
        lists = in_edges(edges)
        g_two, u_one, dws2, dwn2 = backward_layer(
            packed, None, edges, lists, g_three, ws3, pre_two, act_one, agg_one, w_nbr2, wn3_t)
        dws1, dwn1 = backward_layer(
            packed, gather_rows(u_one), edges, lists, g_two, w_self2, pre_one, feat, agg_x, None, None)
        last = jnp.concatenate([v[:, :D // 2] + v[:, D // 2:] for v in (dws3, dwn3)], axis=1)
        loss, *firsts, last_self, last_nbr = lay_out(*reduce_shares([dws1, dwn1, dws2, dwn2, last], loss, 7))
        return (loss.reshape(()), *firsts, last_self.T, last_nbr.T)

    row = P(AX, None)
    return jax.shard_map(
        device_step, mesh=mesh,
        in_specs=(P(None, AX), row, row, row, row, P(), P(), P(), P(), P(AX)),
        out_specs=(P(), row, row, P(), P(), P(), P()),
        check_vma=False)
```

profile of v0, /device:TPU:0, one launch (start us, length us, event | category | flops | bytes accessed | tf_op | source)
XLA Modules:
  0.0 525.7 jit_solution(12058082677591822619)
XLA Ops:
  0.7 1.1 fusion.4
  1.9 1.0 bitcast_select_fusion.1
  2.9 0.8 add_bitcast_fusion
  3.7 0.9 copy.66
  4.6 7.3 %all-to-all-start = ((s32[32,16,128]{2,1,0:T(8,128)}), s32[32,16,128]{2,1,0:T(8,128)S(1)}, u32[]{:S(2)}, u32[]{:S(2)}) async-start(s32[32,16,128]{2,1,0:T(8,128)} %copy.66), calls=%async_computation | async-start | bytes 524288 | tf_op jit(solution)/shard_map/all_to_all | solution.py:608
  12.2 11.2 %sort.14 = (s32[20480]{0:T(1024)S(1)}, s32[20480]{0:T(1024)}) sort(s32[20480]{0:T(1024)S(1)} %reshape.97, s32[20480]{0:T(1024)S(1)} %iota.21), dimensions={0}, to_apply=%region_1.2 | sort | flops 307200 | bytes 327680 | tf_op jit(solution)/shard_map/sort | solution.py:491
  24.4 1.1 pad_maximum_fusion
  25.5 6.0 %all-to-all-start.1 = ((bf16[32,4,2304]{2,1,0:T(4,128)(2,1)}), bf16[32,4,2304]{2,1,0:T(4,128)(2,1)S(1)}, u32[]{:S(2)}, u32[]{:S(2)}) async-start(bf16[32,4,2304]{2,1,0:T(4,128)(2,1)} %pad_maximum_fusion), calls=%async_computation.1 | async-start | bytes 1179648 | tf_op jit(solution)/shard_map/all_to_all | solution.py:604
  31.7 0.6 maximum_bitcast_fusion.rest_1_
  32.3 0.6 pad_add_fusion.1.refs_1_
  33.5 14.7 %all-to-all-done.1 = bf16[32,4,2304]{2,1,0:T(4,128)(2,1)S(1)} async-done(((bf16[32,4,2304]{2,1,0:T(4,128)(2,1)}), bf16[32,4,2304]{2,1,0:T(4,128)(2,1)S(1)}, u32[]{:S(2)}, u32[]{:S(2)}) %all-to-all-start.1) | async-done | bytes 589856 | tf_op jit(solution)/shard_map/all_to_all | solution.py:604
  48.6 62.5 %shard_map.153.tab_hbm = bf16[65536,128]{1,0:T(8,128)(2,1)} custom-call(bf16[2048,128]{1,0:T(8,128)(2,1)S(1)} %bitcast.73), custom_call_target="tpu_custom_call" | custom-call | tf_op jit(solution)/shard_map/pallas_call | solution.py:167
  111.1 20.5 %shard_map.154 = (bf16[2048,128]{1,0:T(8,128)(2,1)S(1)}, f32[2048,128]{1,0:T(8,128)S(1)}, bf16[2048,128]{1,0:T(8,128)(2,1)S(1)}) custom-call(s32[20480]{0:T(1024)S(1)} %bitcast.76, bf16[65536,128]{1,0:T(8,128)(2,1)} %shard_map.153.tab_hbm, bf16[2048,128]{1,0:T(8,128)(2,1)S(1)} %bitcast.74, f32[2048,2]{1,0:T(8,128)S(1)} %copy.70.side_hbm, ...), custom_call_target="tpu_custom_call" | custom-call | tf_op jit(solution)/shard_map/pallas_call | solution.py:277
  131.7 1.0 copy-done.3
  132.7 0.8 copy-done.6
  133.5 62.8 %shard_map.155.tab_hbm = bf16[65536,128]{1,0:T(8,128)(2,1)} custom-call(bf16[2048,128]{1,0:T(8,128)(2,1)S(1)} %get-tuple-element.36.refs_0_.x_hbm.act_hbm), custom_call_target="tpu_custom_call" | custom-call | tf_op jit(solution)/shard_map/pallas_call | solution.py:167
  196.3 20.5 %shard_map.156 = (bf16[2048,128]{1,0:T(8,128)(2,1)S(1)}, f32[2048,128]{1,0:T(8,128)S(1)}, bf16[2048,128]{1,0:T(8,128)(2,1)S(1)}) custom-call(s32[20480]{0:T(1024)S(1)} %bitcast.77, bf16[65536,128]{1,0:T(8,128)(2,1)} %shard_map.155.tab_hbm, bf16[2048,128]{1,0:T(8,128)(2,1)S(1)} %get-tuple-element.36.refs_0_.x_hbm.act_hbm, f32[2048,2]{1,0:T(8,128)S(1)} %copy.70.side_hbm, ...), custom_call_target="tpu_custom_call" | custom-call | tf_op jit(solution)/shard_map/pallas_call | solution.py:277
  216.9 1.0 copy-done.4
  217.9 0.8 copy-done.7
  218.6 62.6 %shard_map.157.tab_hbm = bf16[65536,128]{1,0:T(8,128)(2,1)} custom-call(bf16[2048,128]{1,0:T(8,128)(2,1)S(1)} %get-tuple-element.37.refs_0_.x_hbm), custom_call_target="tpu_custom_call" | custom-call | tf_op jit(solution)/shard_map/pallas_call | solution.py:167
  281.3 22.2 %shard_map.158 = (bf16[1024,128]{1,0:T(8,128)(2,1)S(1)}, f32[128,128]{1,0:T(8,128)S(1)}, f32[128,128]{1,0:T(8,128)S(1)}, f32[8,128]{1,0:T(8,128)S(1)}) custom-call(s32[20480]{0:T(1024)S(1)} %bitcast.78, bf16[65536,128]{1,0:T(8,128)(2,1)} %shard_map.157.tab_hbm, bf16[2048,128]{1,0:T(8,128)(2,1)S(1)} %get-tuple-element.37.refs_0_.x_hbm, ...), custom_call_target="tpu_custom_call" | custom-call | tf_op jit(solution)/shard_map/pallas_call | solution.py:330
  303.5 0.7 copy-done.2
  304.2 47.2 %shard_map.159 = (bf16[32768,128]{1,0:T(8,128)(2,1)}, s32[5376,128]{1,0:T(8,128)}) custom-call(bf16[1024,128]{1,0:T(8,128)(2,1)} %copy-done.2, s32[168,128]{1,0:T(8,128)} %pad_add_fusion.1.refs_1_), custom_call_target="tpu_custom_call" | custom-call | tf_op jit(solution)/shard_map/pallas_call | solution.py:167
  351.9 1.3 copy-done.12
  353.2 4.3 bitcast_select_fusion
  357.5 43.1 %shard_map.160 = (bf16[2048,128]{1,0:T(8,128)(2,1)}, bf16[2048,128]{1,0:T(8,128)(2,1)}, f32[128,128]{1,0:T(8,128)}, f32[128,128]{1,0:T(8,128)}) custom-call(s32[32,168,128]{2,1,0:T(8,128)} %bitcast.79, s32[688128]{0:T(1024)} %get-tuple-element.67.src_hbm, s32[688128]{0:T(1024)} %get-tuple-element.66.dst_hbm, ...), custom_call_target="tpu_custom_call" | custom-call | tf_op jit(solution)/shard_map/pallas_call | solution.py:473
  400.7 1.0 copy-done.8
  401.7 62.7 %shard_map.161.rest_0_ = bf16[65536,128]{1,0:T(8,128)(2,1)} custom-call(bf16[2048,128]{1,0:T(8,128)(2,1)S(1)} %copy-done.8), custom_call_target="tpu_custom_call" | custom-call | tf_op jit(solution)/shard_map/pallas_call | solution.py:167
  464.5 0.7 pad_maximum_fusion.3.refs_4_
  465.3 39.6 %shard_map.162 = (f32[128,128]{1,0:T(8,128)}, f32[128,128]{1,0:T(8,128)}) custom-call(s32[32,168,128]{2,1,0:T(8,128)} %bitcast.80, s32[688128]{0:T(1024)} %get-tuple-element.67.src_hbm, s32[688128]{0:T(1024)} %get-tuple-element.66.dst_hbm, bf16[32768,128]{1,0:T(8,128)(2,1)} %get-tuple-element.41.packed_hbm, bf16[2048,128]{1,0:T(8,128)(2,1)} %get-tuple-element.44.gu_hbm, ...), custom_call_target="tpu_custom_call" | custom-call | tf_op jit(solution)/shard_map/pallas_call | solution.py:473
  504.9 19.1 %reduce_shares.1 = (f32[8,128]{1,0:T(8,128)}, f32[32,16,128]{2,1,0:T(8,128)}) custom-call(f32[128,128]{1,0:T(8,128)} %get-tuple-element.48.refs_0_, f32[128,128]{1,0:T(8,128)} %get-tuple-element.49.refs_1_, f32[128,128]{1,0:T(8,128)} %get-tuple-element.50.refs_2_, f32[128,128]{1,0:T(8,128)} %get-tuple-element.51.refs_3_, ...), custom_call_target="tpu_custom_call" | custom-call | tf_op jit(solution)/shard_map/reduce_shares/pallas_call | solution.py:569
  524.0 1.7 lay_out.1
  (65 shorter events, 3.0 us)
Async XLA Ops:
  0.6 11.3 %copy-start.15 = (bf16[128,40]{0,1:T(8,128)(2,1)S(1)}, bf16[128,40]{0,1:T(8,128)(2,1)}, u32[]{:S(2)}) copy-start(bf16[128,40]{0,1:T(8,128)(2,1)} %param.17) | copy-start | bytes 30724
  0.6 11.5 %copy-start.14 = (bf16[128,40]{0,1:T(8,128)(2,1)S(1)}, bf16[128,40]{0,1:T(8,128)(2,1)}, u32[]{:S(2)}) copy-start(bf16[128,40]{0,1:T(8,128)(2,1)} %param.18) | copy-start | bytes 30724
  0.7 22.8 %copy-start.13 = (bf16[65536,4]{0,1:T(4,128)(2,1)S(1)}, bf16[65536,4]{0,1:T(4,128)(2,1)}, u32[]{:S(2)}) copy-start(bf16[65536,4]{0,1:T(4,128)(2,1)} %param.10) | copy-start | bytes 1572868
  3.6 20.2 %copy-start.16 = (bf16[4,128]{1,0:T(4,128)(2,1)S(1)}, bf16[4,128]{1,0:T(4,128)(2,1)}, u32[]{:S(2)}) copy-start(bf16[4,128]{1,0:T(4,128)(2,1)} %param.12) | copy-start | bytes 3076
  3.7 20.2 %copy-start.17 = (bf16[4,128]{1,0:T(4,128)(2,1)S(1)}, bf16[4,128]{1,0:T(4,128)(2,1)}, u32[]{:S(2)}) copy-start(bf16[4,128]{1,0:T(4,128)(2,1)} %param.11) | copy-start | bytes 3076
  4.6 20.9 %all-to-all-start = ((s32[32,16,128]{2,1,0:T(8,128)}), s32[32,16,128]{2,1,0:T(8,128)S(1)}, u32[]{:S(2)}, u32[]{:S(2)}) async-start(s32[32,16,128]{2,1,0:T(8,128)} %copy.66), calls=%async_computation | async-start | bytes 524288 | tf_op jit(solution)/shard_map/all_to_all | solution.py:608
  23.9 257.4 %copy-start.5 = (bf16[2,128,128]{2,1,0:T(8,128)(2,1)}, bf16[2,128,128]{2,1,0:T(8,128)(2,1)S(1)}, u32[]{:S(2)}) copy-start(bf16[2,128,128]{2,1,0:T(8,128)(2,1)S(1)} %pad_maximum_fusion.1.ws_ref) | copy-start | bytes 196612
  25.5 22.6 %all-to-all-start.1 = ((bf16[32,4,2304]{2,1,0:T(4,128)(2,1)}), bf16[32,4,2304]{2,1,0:T(4,128)(2,1)S(1)}, u32[]{:S(2)}, u32[]{:S(2)}) async-start(bf16[32,4,2304]{2,1,0:T(4,128)(2,1)} %pad_maximum_fusion), calls=%async_computation.1 | async-start | bytes 1179648 | tf_op jit(solution)/shard_map/all_to_all | solution.py:604
  48.6 62.5 %copy-start = (bf16[128,2048]{0,1:T(8,128)(2,1)}, bf16[128,2048]{0,1:T(8,128)(2,1)S(1)}, u32[]{:S(2)}) copy-start(bf16[128,2048]{0,1:T(8,128)(2,1)S(1)} %copy.76) | copy-start | bytes 1572868
  131.7 1.0 copy-start.3
  132.7 0.8 copy-start.6
  133.5 62.8 %copy-start.1 = (bf16[2048,128]{1,0:T(8,128)(2,1)}, bf16[2048,128]{1,0:T(8,128)(2,1)S(1)}, u32[]{:S(2)}) copy-start(bf16[2048,128]{1,0:T(8,128)(2,1)S(1)} %get-tuple-element.36.refs_0_.x_hbm.act_hbm) | copy-start | bytes 1572868
  133.5 62.8 %copy-start.9 = (bf16[128,128]{1,0:T(8,128)(2,1)S(1)}, bf16[128,128]{1,0:T(8,128)(2,1)}, u32[]{:S(2)}) copy-start(bf16[128,128]{1,0:T(8,128)(2,1)} %rest_0_.1) | copy-start | bytes 98308
  133.5 62.8 %copy-start.10 = (bf16[128,128]{1,0:T(8,128)(2,1)S(1)}, bf16[128,128]{1,0:T(8,128)(2,1)}, u32[]{:S(2)}) copy-start(bf16[128,128]{1,0:T(8,128)(2,1)} %ws_ref.3) | copy-start | bytes 98308
  216.9 1.0 copy-start.4
  217.9 0.8 copy-start.7
  303.5 0.7 copy-start.2
  304.2 53.3 %copy-start.11 = (f32[8,128]{1,0:T(8,128)}, f32[8,128]{1,0:T(8,128)S(1)}, u32[]{:S(2)}) copy-start(f32[8,128]{1,0:T(8,128)S(1)} %get-tuple-element.54.refs_5_) | copy-start | bytes 12292
  351.4 1.8 copy-start.12
  400.7 1.0 copy-start.8
where the time goes:
time: 526 us
  Pallas kernels  465 us (88%)
  other arithmetic  22.1 us (4%)
  waiting for transfers between devices  14.7 us (3%)
  starting transfers between devices  13.3 us (3%)
  local copies, waits for them, and re-layouts  9.71 us (2%)
    pallas_call x5, Pallas kernels, all_gather(): pl.pallas_call(kernel, out_shape=[jax.ShapeDtypeStruct((v.shape[0] * NDEV...  298 us
    pallas_call x2, Pallas kernels, backward_layer(): pl.pallas_call(kernel, out_shape=outs, in_specs=specs, out_specs=[vm] * l...  82.7 us
    pallas_call x2, Pallas kernels, hidden_layer(): pl.pallas_call(kernel, out_shape=[jax.ShapeDtypeStruct((R, D), BF), jax.S...  41.1 us
    pallas_call x1, Pallas kernels, output_layer(): pl.pallas_call(kernel, out_shape=[jax.ShapeDtypeStruct((HALF, D), BF), ja...  22.2 us
    pallas_call x1, Pallas kernels, reduce_shares(): pl.pallas_call(kernel, name='reduce_shares', out_shape=[jax.ShapeDtypeStr...  19.1 us
    all_to_all x1, waiting for transfers between devices, device_step(): in_coming = lax.all_to_all(out_going, AX, 0, 0, tiled=True)  14.7 us
    sort x1, other arithmetic, sorted_edges(): key = lax.sort(key.reshape(E))  11.2 us
  transfers between devices with their start and end apart: 2, of which 1 were waited for; matrix products, arithmetic and copies ran while one was open for 3% of the time, Pallas kernels for 0%

commit v1 on v0

--- a/solution.py
+++ b/solution.py
@@ -20,12 +20,13 @@
 SLOTS = 8
 TBUF = 10
 BBUF = 8
-UNROLL = 32
+UNROLL = 64
 MESH = pl.DeviceIdType.MESH
 VMEM = pltpu.VMEM
 BF = jnp.bfloat16
 F32 = jnp.float32
 VLIM = 62 * 1024 * 1024
+BLIM = 53 * 1024 * 1024
 LLIM = 46 * 1024 * 1024
 GLIM = 48 * 1024 * 1024
 
@@ -475,7 +476,7 @@
         scratch_shapes=[VMEM((R + 8, D), F32)] * NACC + [pltpu.SMEM((NDEV, D), jnp.int32)] + [pltpu.SMEM((SLOTS * CAP,), jnp.int32)] * 2
         + [pltpu.SemaphoreType.DMA((2, SLOTS)), VMEM((N, D), F32), VMEM((D, 2 * D), BF)]
         + [VMEM(v.shape, v.dtype) for v in (g_up, pre, act, agg)] + [pltpu.SemaphoreType.DMA((5,))] + stage,
-        compiler_params=pltpu.CompilerParams(vmem_limit_bytes=VLIM))(*args)
+        compiler_params=pltpu.CompilerParams(vmem_limit_bytes=BLIM))(*args)
 
 
 def rank(j):

time: 526 us -> 525 us (level)
  no operation moved by 1% of the time
where the time goes in v1:
time: 525 us
  Pallas kernels  462 us (88%)
  other arithmetic  21.5 us (4%)
  waiting for transfers between devices  15.3 us (3%)
  starting transfers between devices  13.3 us (3%)
  local copies, waits for them, and re-layouts  11.6 us (2%)
    pallas_call x5, Pallas kernels, all_gather(): pl.pallas_call(kernel, out_shape=[jax.ShapeDtypeStruct((v.shape[0] * NDEV...  298 us
    pallas_call x2, Pallas kernels, backward_layer(): pl.pallas_call(kernel, out_shape=outs, in_specs=specs, out_specs=[vm] * l...  80.4 us
    pallas_call x2, Pallas kernels, hidden_layer(): pl.pallas_call(kernel, out_shape=[jax.ShapeDtypeStruct((R, D), BF), jax.S...  40.6 us
    pallas_call x1, Pallas kernels, output_layer(): pl.pallas_call(kernel, out_shape=[jax.ShapeDtypeStruct((HALF, D), BF), ja...  21.9 us
    pallas_call x1, Pallas kernels, reduce_shares(): pl.pallas_call(kernel, name='reduce_shares', out_shape=[jax.ShapeDtypeStr...  19.1 us
    all_to_all x1, waiting for transfers between devices, device_step(): in_coming = lax.all_to_all(out_going, AX, 0, 0, tiled=True)  15.3 us
    sort x1, other arithmetic, sorted_edges(): key = lax.sort(key.reshape(E))  11.2 us
  transfers between devices with their start and end apart: 2, of which 1 were waited for; matrix products, arithmetic and copies ran while one was open for 3% of the time, Pallas kernels for 0%

profile of v1, /device:TPU:0, one launch (start us, length us, event | category | flops | bytes accessed | tf_op | source)
XLA Modules:
  0.0 524.5 jit_solution(4443595932397336600)
XLA Ops:
  0.7 1.1 fusion.4
  1.9 1.0 bitcast_select_fusion.1
  2.9 0.8 add_bitcast_fusion
  3.7 0.9 copy.66
  4.6 7.3 %all-to-all-start = ((s32[32,16,128]{2,1,0:T(8,128)}), s32[32,16,128]{2,1,0:T(8,128)S(1)}, u32[]{:S(2)}, u32[]{:S(2)}) async-start(s32[32,16,128]{2,1,0:T(8,128)} %copy.66), calls=%async_computation | async-start | bytes 524288 | tf_op jit(solution)/shard_map/all_to_all | solution.py:609
  12.2 11.2 %sort.14 = (s32[20480]{0:T(1024)S(1)}, s32[20480]{0:T(1024)}) sort(s32[20480]{0:T(1024)S(1)} %reshape.97, s32[20480]{0:T(1024)S(1)} %iota.21), dimensions={0}, to_apply=%region_1.2 | sort | flops 307200 | bytes 327680 | tf_op jit(solution)/shard_map/sort | solution.py:492
  24.4 1.1 pad_maximum_fusion
  25.5 6.0 %all-to-all-start.1 = ((bf16[32,4,2304]{2,1,0:T(4,128)(2,1)}), bf16[32,4,2304]{2,1,0:T(4,128)(2,1)S(1)}, u32[]{:S(2)}, u32[]{:S(2)}) async-start(bf16[32,4,2304]{2,1,0:T(4,128)(2,1)} %pad_maximum_fusion), calls=%async_computation.1 | async-start | bytes 1179648 | tf_op jit(solution)/shard_map/all_to_all | solution.py:605
  31.7 0.6 pad_add_fusion.1.refs_1_
  32.8 15.3 %all-to-all-done.1 = bf16[32,4,2304]{2,1,0:T(4,128)(2,1)S(1)} async-done(((bf16[32,4,2304]{2,1,0:T(4,128)(2,1)}), bf16[32,4,2304]{2,1,0:T(4,128)(2,1)S(1)}, u32[]{:S(2)}, u32[]{:S(2)}) %all-to-all-start.1) | async-done | bytes 589856 | tf_op jit(solution)/shard_map/all_to_all | solution.py:605
  48.6 62.5 %shard_map.153.tab_hbm = bf16[65536,128]{1,0:T(8,128)(2,1)} custom-call(bf16[2048,128]{1,0:T(8,128)(2,1)S(1)} %bitcast.73), custom_call_target="tpu_custom_call" | custom-call | tf_op jit(solution)/shard_map/pallas_call | solution.py:168
  111.1 20.3 %shard_map.154 = (bf16[2048,128]{1,0:T(8,128)(2,1)S(1)}, f32[2048,128]{1,0:T(8,128)S(1)}, bf16[2048,128]{1,0:T(8,128)(2,1)S(1)}) custom-call(s32[20480]{0:T(1024)S(1)} %bitcast.76, bf16[65536,128]{1,0:T(8,128)(2,1)} %shard_map.153.tab_hbm, bf16[2048,128]{1,0:T(8,128)(2,1)S(1)} %bitcast.74, f32[2048,2]{1,0:T(8,128)S(1)} %copy.70.side_hbm, ...), custom_call_target="tpu_custom_call" | custom-call | tf_op jit(solution)/shard_map/pallas_call | solution.py:278
  131.4 1.0 copy-done.4
  132.4 0.8 copy-done.6
  133.2 62.8 %shard_map.155.tab_hbm = bf16[65536,128]{1,0:T(8,128)(2,1)} custom-call(bf16[2048,128]{1,0:T(8,128)(2,1)S(1)} %get-tuple-element.36.refs_0_.x_hbm.act_hbm), custom_call_target="tpu_custom_call" | custom-call | tf_op jit(solution)/shard_map/pallas_call | solution.py:168
  196.1 20.3 %shard_map.156 = (bf16[2048,128]{1,0:T(8,128)(2,1)S(1)}, f32[2048,128]{1,0:T(8,128)S(1)}, bf16[2048,128]{1,0:T(8,128)(2,1)S(1)}) custom-call(s32[20480]{0:T(1024)S(1)} %bitcast.77, bf16[65536,128]{1,0:T(8,128)(2,1)} %shard_map.155.tab_hbm, bf16[2048,128]{1,0:T(8,128)(2,1)S(1)} %get-tuple-element.36.refs_0_.x_hbm.act_hbm, f32[2048,2]{1,0:T(8,128)S(1)} %copy.70.side_hbm, ...), custom_call_target="tpu_custom_call" | custom-call | tf_op jit(solution)/shard_map/pallas_call | solution.py:278
  216.4 0.9 copy-done.5
  217.3 0.8 copy-done.8
  218.1 62.6 %shard_map.157.tab_hbm = bf16[65536,128]{1,0:T(8,128)(2,1)} custom-call(bf16[2048,128]{1,0:T(8,128)(2,1)S(1)} %get-tuple-element.37.refs_0_.x_hbm), custom_call_target="tpu_custom_call" | custom-call | tf_op jit(solution)/shard_map/pallas_call | solution.py:168
  280.8 21.9 %shard_map.158 = (bf16[1024,128]{1,0:T(8,128)(2,1)S(1)}, f32[128,128]{1,0:T(8,128)S(1)}, f32[128,128]{1,0:T(8,128)S(1)}, f32[8,128]{1,0:T(8,128)S(1)}) custom-call(s32[20480]{0:T(1024)S(1)} %bitcast.78, bf16[65536,128]{1,0:T(8,128)(2,1)} %shard_map.157.tab_hbm, bf16[2048,128]{1,0:T(8,128)(2,1)S(1)} %get-tuple-element.37.refs_0_.x_hbm, ...), custom_call_target="tpu_custom_call" | custom-call | tf_op jit(solution)/shard_map/pallas_call | solution.py:331
  302.7 0.7 copy-done.2
  303.4 47.2 %shard_map.159 = (bf16[32768,128]{1,0:T(8,128)(2,1)}, s32[5376,128]{1,0:T(8,128)}) custom-call(bf16[1024,128]{1,0:T(8,128)(2,1)} %copy-done.2, s32[168,128]{1,0:T(8,128)} %pad_add_fusion.1.refs_1_), custom_call_target="tpu_custom_call" | custom-call | tf_op jit(solution)/shard_map/pallas_call | solution.py:168
  351.2 1.3 copy-done.17
  352.5 4.3 bitcast_select_fusion
  356.8 42.4 %shard_map.160 = (bf16[2048,128]{1,0:T(8,128)(2,1)}, bf16[2048,128]{1,0:T(8,128)(2,1)}, f32[128,128]{1,0:T(8,128)S(1)}, f32[128,128]{1,0:T(8,128)S(1)}) custom-call(s32[32,168,128]{2,1,0:T(8,128)} %bitcast.79, s32[688128]{0:T(1024)} %get-tuple-element.67.src_hbm, s32[688128]{0:T(1024)} %get-tuple-element.66.dst_hbm, ...), custom_call_target="tpu_custom_call" | custom-call | tf_op jit(solution)/shard_map/pallas_call | solution.py:474
  399.8 1.1 copy-done.9
  400.9 62.7 %shard_map.161.rest_0_ = bf16[65536,128]{1,0:T(8,128)(2,1)} custom-call(bf16[2048,128]{1,0:T(8,128)(2,1)S(1)} %copy-done.9), custom_call_target="tpu_custom_call" | custom-call | tf_op jit(solution)/shard_map/pallas_call | solution.py:168
  463.7 0.7 pad_maximum_fusion.3.refs_4_
  464.4 38.0 %shard_map.162 = (f32[128,128]{1,0:T(8,128)S(1)}, f32[128,128]{1,0:T(8,128)S(1)}) custom-call(s32[32,168,128]{2,1,0:T(8,128)} %bitcast.80, s32[688128]{0:T(1024)} %get-tuple-element.67.src_hbm, s32[688128]{0:T(1024)} %get-tuple-element.66.dst_hbm, bf16[32768,128]{1,0:T(8,128)(2,1)} %get-tuple-element.41.packed_hbm, bf16[2048,128]{1,0:T(8,128)(2,1)S(1)} %copy-done.7, ...), custom_call_target="tpu_custom_call" | custom-call | tf_op jit(solution)/shard_map/pallas_call | solution.py:474
  503.1 0.6 copy-done.15
  503.7 19.1 %reduce_shares.1 = (f32[8,128]{1,0:T(8,128)}, f32[32,16,128]{2,1,0:T(8,128)}) custom-call(f32[128,128]{1,0:T(8,128)} %copy-done.14, f32[128,128]{1,0:T(8,128)} %copy-done.15, f32[128,128]{1,0:T(8,128)} %copy-done.12, f32[128,128]{1,0:T(8,128)} %copy-done.13, f32[128,128]{1,0:T(8,128)} %pad_maximum_fusion.3.refs_4_, f32[8,128]{1,0:T(8,128)} %copy-done.16), custom_call_target="tpu_custom_call" | custom-call | tf_op jit(solution)/shard_map/reduce_shares/pallas_call | solution.py:570
  522.9 1.7 lay_out.1
  (75 shorter events, 4.2 us)
Async XLA Ops:
  0.6 11.3 %copy-start.20 = (bf16[128,40]{0,1:T(8,128)(2,1)S(1)}, bf16[128,40]{0,1:T(8,128)(2,1)}, u32[]{:S(2)}) copy-start(bf16[128,40]{0,1:T(8,128)(2,1)} %param.17) | copy-start | bytes 30724
  0.6 11.5 %copy-start.19 = (bf16[128,40]{0,1:T(8,128)(2,1)S(1)}, bf16[128,40]{0,1:T(8,128)(2,1)}, u32[]{:S(2)}) copy-start(bf16[128,40]{0,1:T(8,128)(2,1)} %param.18) | copy-start | bytes 30724
  0.7 22.8 %copy-start.18 = (bf16[65536,4]{0,1:T(4,128)(2,1)S(1)}, bf16[65536,4]{0,1:T(4,128)(2,1)}, u32[]{:S(2)}) copy-start(bf16[65536,4]{0,1:T(4,128)(2,1)} %param.10) | copy-start | bytes 1572868
  3.6 20.2 %copy-start.21 = (bf16[4,128]{1,0:T(4,128)(2,1)S(1)}, bf16[4,128]{1,0:T(4,128)(2,1)}, u32[]{:S(2)}) copy-start(bf16[4,128]{1,0:T(4,128)(2,1)} %param.12) | copy-start | bytes 3076
  3.7 20.2 %copy-start.22 = (bf16[4,128]{1,0:T(4,128)(2,1)S(1)}, bf16[4,128]{1,0:T(4,128)(2,1)}, u32[]{:S(2)}) copy-start(bf16[4,128]{1,0:T(4,128)(2,1)} %param.11) | copy-start | bytes 3076
  4.6 20.9 %all-to-all-start = ((s32[32,16,128]{2,1,0:T(8,128)}), s32[32,16,128]{2,1,0:T(8,128)S(1)}, u32[]{:S(2)}, u32[]{:S(2)}) async-start(s32[32,16,128]{2,1,0:T(8,128)} %copy.66), calls=%async_computation | async-start | bytes 524288 | tf_op jit(solution)/shard_map/all_to_all | solution.py:609
  25.5 22.6 %all-to-all-start.1 = ((bf16[32,4,2304]{2,1,0:T(4,128)(2,1)}), bf16[32,4,2304]{2,1,0:T(4,128)(2,1)S(1)}, u32[]{:S(2)}, u32[]{:S(2)}) async-start(bf16[32,4,2304]{2,1,0:T(4,128)(2,1)} %pad_maximum_fusion), calls=%async_computation.1 | async-start | bytes 1179648 | tf_op jit(solution)/shard_map/all_to_all | solution.py:605
  48.6 62.5 %copy-start = (bf16[128,2048]{0,1:T(8,128)(2,1)}, bf16[128,2048]{0,1:T(8,128)(2,1)S(1)}, u32[]{:S(2)}) copy-start(bf16[128,2048]{0,1:T(8,128)(2,1)S(1)} %copy.76) | copy-start | bytes 1572868
  131.4 1.0 copy-start.4
  132.4 0.8 copy-start.6
  133.2 62.8 %copy-start.1 = (bf16[2048,128]{1,0:T(8,128)(2,1)}, bf16[2048,128]{1,0:T(8,128)(2,1)S(1)}, u32[]{:S(2)}) copy-start(bf16[2048,128]{1,0:T(8,128)(2,1)S(1)} %get-tuple-element.36.refs_0_.x_hbm.act_hbm) | copy-start | bytes 1572868
  133.2 62.8 %copy-start.10 = (bf16[128,128]{1,0:T(8,128)(2,1)S(1)}, bf16[128,128]{1,0:T(8,128)(2,1)}, u32[]{:S(2)}) copy-start(bf16[128,128]{1,0:T(8,128)(2,1)} %rest_0_.1) | copy-start | bytes 98308
  133.2 62.8 %copy-start.11 = (bf16[128,128]{1,0:T(8,128)(2,1)S(1)}, bf16[128,128]{1,0:T(8,128)(2,1)}, u32[]{:S(2)}) copy-start(bf16[128,128]{1,0:T(8,128)(2,1)} %ws_ref.3) | copy-start | bytes 98308
  216.4 1.0 copy-start.5
  217.3 0.8 copy-start.8
  302.7 0.7 copy-start.2
  303.4 53.3 %copy-start.16 = (f32[8,128]{1,0:T(8,128)}, f32[8,128]{1,0:T(8,128)S(1)}, u32[]{:S(2)}) copy-start(f32[8,128]{1,0:T(8,128)S(1)} %get-tuple-element.54.refs_5_) | copy-start | bytes 12292
  350.7 1.8 copy-start.17
  352.5 4.3 copy-start.3
  399.2 0.6 copy-start.12
  399.8 63.8 %copy-start.13 = (f32[128,128]{1,0:T(8,128)}, f32[128,128]{1,0:T(8,128)S(1)}, u32[]{:S(2)}) copy-start(f32[128,128]{1,0:T(8,128)S(1)} %get-tuple-element.51.refs_3_) | copy-start | bytes 196612
  399.8 1.1 copy-start.9
  400.9 63.5 %copy-start.7 = (bf16[2048,128]{1,0:T(8,128)(2,1)S(1)}, bf16[2048,128]{1,0:T(8,128)(2,1)}, u32[]{:S(2)}) copy-start(bf16[2048,128]{1,0:T(8,128)(2,1)} %get-tuple-element.44.gu_hbm) | copy-start | bytes 1572868
  502.5 0.6 copy-start.14
  503.1 0.6 copy-start.15
